TPU v7x, 512 devices: a whole 4x8x8 slice. The times are simulated.
512 devices in a mesh: row: 16 (over y_lo, z), col: 8 (over x, core), dp: 4 (over y_hi).
Axes of the slice: x: 4, y: 8 (y_hi: 4, y_lo: 2; y = y_hi * 2 + y_lo), z: 8, core: 2. Of those that a mesh axis runs over, the one named last changes fastest.
Arguments:
- tokens: bfloat16 [1536, 6144], P('dp', 'row'), parts along dimension 0, may hold values from -120 to 120
- norm_gain: float32 [6144], P('row'), may hold values from 0.25 to 1.75
- qkv_weight: bfloat16 [6144, 3, 3072], P('row', None, 'col'), may hold values from -2.5 to 2.5
- out_weight: bfloat16 [3072, 6144], P('col', 'row'), may hold values from -0.109375 to 0.109375
Outputs:
- projected: bfloat16 [1536, 6144], P('dp', 'row'), parts along dimension 0
There are 4 independent parts, one for each index of `dp`. A program takes and returns all parts, laid end to end along the dimension named above; an argument that names none is the same for every part. Nothing has to cross between parts.
All inputs are finite; a program needn't handle non-finite values.
Results may differ from a plain program's by a relative error of at most 0.025.
Values may be sent and summed in bfloat16 or wider, within the bound.
No kernel may reach another device: no remote copies, remote signals or barrier semaphores. Data moves between devices by JAX's collectives and lax.ppermute only.
A program may use at most 64 MiB of HBM per device.

v0:
```python
import math

import jax
import jax.numpy as jnp
from jax import lax
from jax.sharding import PartitionSpec as P

K = 128


EPSILON = 1e-05


def copy_for_each(shard, axis):
    devices = lax.axis_size(axis)
    return lax.all_to_all(
        jnp.broadcast_to(shard[None], (devices, *shard.shape)), axis, 0, 0, tiled=True
    )


def over_copies(shard, axis):
    everything = copy_for_each(shard, axis)
    return jnp.sum(everything, axis=0)


def together(arrays, axis):
    ends = [0]
    for a in arrays:
        ends.append(ends[-1] + a.size)
    running = over_copies(jnp.concatenate([a.ravel() for a in arrays]), axis)
    return tuple((running[b:e].reshape(a.shape) for a, b, e in zip(arrays, ends, ends[1:])))


def filled_up(lines, devices):
    spare = -len(lines) % devices
    return jnp.pad(lines, [(0, spare)] + [(0, 0)] * (lines.ndim - 1))


def laid_out(parts, dim):
    lengths = list(parts.shape[1:])
    lengths[dim] *= parts.shape[0]
    return jnp.moveaxis(parts, 0, dim).reshape(lengths)


def gather_directly(shard, axis, dim):
    parts = copy_for_each(shard, axis)
    return laid_out(parts, dim)


def split_up(shard, dim, devices):
    lengths = shard.shape
    parts = shard.reshape(*lengths[:dim], devices, lengths[dim] // devices, *lengths[dim + 1 :])
    return jnp.moveaxis(parts, dim, 0)


def summed_on_arrival(shard, axis, dim):
    parts = split_up(shard, dim, lax.axis_size(axis))
    arrived = lax.all_to_all(parts, axis, split_axis=0, concat_axis=0, tiled=True)
    return arrived.astype(jnp.float32).sum(axis=0)


def nested_sum(shard, axes):
    lines = shard.reshape(-1, shard.shape[-1])
    padded = filled_up(lines, lax.axis_size(axes))
    whole = gather_directly(summed_on_arrival(padded, axes, 0).astype(jnp.bfloat16), axes, 0)
    return lax.slice_in_dim(whole, 0, len(lines)).reshape(shard.shape).astype(jnp.float32)


def over_copies_2(shard, axis):
    everything = copy_for_each(shard, axis)
    return jnp.sum(everything.astype(jnp.float32), axis=0)


def attend(queries, key_rows, value_rows):
    query_total = queries.shape[0]
    head_count = queries.shape[1] // K
    scaling = 1.0 / math.sqrt(K)
    split_keys = key_rows.reshape(key_rows.shape[0], head_count, K)
    split_values = value_rows.reshape(value_rows.shape[0], head_count, K)
    split_queries = queries.reshape(query_total, head_count, K)
    scores = (
        jnp.einsum("qhd,khd->hqk", split_queries, split_keys, preferred_element_type=jnp.float32)
        * scaling
    )
    largest = jnp.max(scores, axis=2, keepdims=True)
    exponent = jnp.exp(scores - largest)
    softmax_weights = (exponent / jnp.sum(exponent, axis=2, keepdims=True)).astype(jnp.bfloat16)
    mixed = jnp.einsum(
        "hqk,khd->qhd", softmax_weights, split_values, preferred_element_type=jnp.float32
    )
    result = mixed.astype(jnp.bfloat16)
    return result.reshape(query_total, head_count * K)


def shards(tokens, norm_gain, qkv_weight, out_weight):
    row_count, block_width = tokens.shape
    full_width = block_width * lax.axis_size("row")
    values = tokens.astype(jnp.float32)
    totals, squares = together(
        (jnp.sum(values, axis=1, keepdims=True), jnp.sum(values * values, axis=1, keepdims=True)),
        "row",
    )
    average = totals / full_width
    variance = squares / full_width - average * average
    centered = values - average
    normed = (centered * lax.rsqrt(variance + EPSILON) * norm_gain).astype(jnp.bfloat16)
    head_columns = qkv_weight.shape[2]
    partial_value = jnp.dot(
        normed,
        qkv_weight.reshape(block_width, 3 * head_columns),
        preferred_element_type=jnp.float32,
    )
    summed = (
        nested_sum(partial_value.astype(jnp.bfloat16), "row")
        .astype(jnp.bfloat16)
        .reshape(row_count, 3, head_columns)
    )
    attended = attend(summed[:, 0], summed[:, 1], summed[:, 2])
    partial_out = jnp.dot(attended, out_weight, preferred_element_type=jnp.float32)
    return (
        over_copies_2(partial_out.astype(jnp.bfloat16), "col")
        .astype(jnp.float32)
        .astype(jnp.bfloat16)
    )


def solution(mesh):
    in_specs = (P("dp", "row"), P("row"), P("row", None, "col"), P("col", "row"))
    out_specs = P("dp", "row")
    return jax.shard_map(shards, mesh=mesh, in_specs=in_specs, out_specs=out_specs, check_vma=False)
```

profile of v0, /device:TPU:1, one launch (start us, length us, event | category | flops | bytes accessed | tf_op | source)
XLA Modules:
  0.0 117.2 jit_solution(6283614068841369683)
XLA Ops:
  0.0 0.0 copy-start
  0.0 0.0 copy-start.1
  0.0 0.0 copy-start.2
  0.0 1.2 %convert_reduce_fusion = (f32[384]{0:T(512)S(1)}, f32[384]{0:T(512)S(1)}) fusion(bf16[384,384]{1,0:T(8,128)(2,1)} %param.4), kind=kLoop, calls=%fused_computation.11 | loop fusion | flops 589056 | bytes 297984 | tf_op jit(solution)/shard_map/reduce_sum | solution.py:100
  1.2 0.6 broadcast_in_dim.6
  1.9 12.0 %all-to-all-start = ((f32[16,1,768]{2,1,0:T(1,128)}), f32[16,1,768]{2,1,0:T(1,128)S(1)}, u32[]{:S(2)}, u32[]{:S(2)}) async-start(f32[16,1,768]{2,1,0:T(1,128)} %broadcast_in_dim.6), calls=%async_computation | async-start | bytes 98304 | tf_op jit(solution)/shard_map/all_to_all | solution.py:16
  13.9 2.5 %copy.21 = bf16[384,3,384]{0,2,1:T(8,128)(2,1)S(1)} copy(bf16[384,3,384]{2,0,1:T(8,128)(2,1)} %param.6) | data formatting | bytes 1769472 | tf_op args[2]
  16.4 4.9 %all-to-all-done = f32[16,1,768]{2,1,0:T(1,128)S(1)} async-done(((f32[16,1,768]{2,1,0:T(1,128)}), f32[16,1,768]{2,1,0:T(1,128)S(1)}, u32[]{:S(2)}, u32[]{:S(2)}) %all-to-all-start) | async-done | bytes 49184 | tf_op jit(solution)/shard_map/all_to_all | solution.py:16
  21.3 0.0 copy-done.1
  21.3 0.0 copy-done.2
  21.3 0.7 convolution_convert_fusion
  22.0 23.1 %all_to_all.21 = bf16[16,24,1152]{2,1,0:T(8,128)(2,1)S(1)} all-to-all(bf16[16,24,1152]{2,1,0:T(8,128)(2,1)S(1)} %bitcast.15), channel_id=1, replica_groups=mesh['row'=16,'col'=8,'dp'=4] {'row'}, dimensions={0} | all-to-all | bytes 1769472 | tf_op jit(solution)/shard_map/all_to_all | solution.py:58
  45.1 0.1 reduce_sum.63
  45.2 0.1 broadcast_in_dim.7
  45.3 29.1 %all_to_all.22 = bf16[16,24,1152]{2,1,0:T(8,128)(2,1)S(1)} all-to-all(bf16[16,24,1152]{2,1,0:T(8,128)(2,1)S(1)} %broadcast_in_dim.7), channel_id=1, replica_groups=mesh['row'=16,'col'=8,'dp'=4] {'row'}, dimensions={0} | all-to-all | bytes 1769472 | tf_op jit(solution)/shard_map/all_to_all | solution.py:16
  74.4 0.3 reshape.37
  74.7 1.2 %fusion.14 = (bf16[384,1,384]{2,1,0:T(2,128)(2,1)S(1)}, bf16[384,1,384]{2,1,0:T(2,128)(2,1)S(1)}, bf16[384,1,384]{2,1,0:T(2,128)(2,1)S(1)}) fusion(bf16[384,3,384]{2,1,0:T(4,128)(2,1)S(1)} %reshape.37), kind=kLoop, calls=%fused_computation.24 | loop fusion | bytes 1769472 | tf_op jit(solution)/shard_map/slice | solution.py:118
  76.0 0.9 copy.24
  76.8 0.9 copy.23
  77.7 0.9 copy.22
  78.5 0.8 fusion.15
  79.3 0.4 convolution_convert_fusion.2
  79.7 0.0 copy-done
  79.7 0.4 convolution_convert_fusion.1
  80.0 0.2 broadcast_in_dim.8
  80.2 35.9 %all_to_all.23 = bf16[8,384,384]{2,1,0:T(8,128)(2,1)S(1)} all-to-all(bf16[8,384,384]{2,1,0:T(8,128)(2,1)S(1)} %broadcast_in_dim.8), channel_id=1, replica_groups=mesh['row'=16,'col'=8,'dp'=4] {'col'}, dimensions={0} | all-to-all | bytes 4718592 | tf_op jit(solution)/shard_map/all_to_all | solution.py:16
  116.1 1.1 reduce_sum.65
  (3 shorter events, 0.1 us)
Async XLA Ops:
  0.0 79.7 %copy-start = (bf16[384,384]{1,0:T(8,128)(2,1)S(1)}, bf16[384,384]{1,0:T(8,128)(2,1)}, u32[]{:S(2)}) copy-start(bf16[384,384]{1,0:T(8,128)(2,1)} %param.7) | copy-start | bytes 884740
  0.0 21.3 %copy-start.1 = (bf16[384,384]{1,0:T(8,128)(2,1)S(1)}, bf16[384,384]{1,0:T(8,128)(2,1)}, u32[]{:S(2)}) copy-start(bf16[384,384]{1,0:T(8,128)(2,1)} %param.4) | copy-start | bytes 884740
  0.0 21.3 %copy-start.2 = (f32[384]{0:T(512)S(1)}, f32[384]{0:T(512)}, u32[]{:S(2)}) copy-start(f32[384]{0:T(512)} %param.5) | copy-start | bytes 4612
  1.9 19.3 %all-to-all-start = ((f32[16,1,768]{2,1,0:T(1,128)}), f32[16,1,768]{2,1,0:T(1,128)S(1)}, u32[]{:S(2)}, u32[]{:S(2)}) async-start(f32[16,1,768]{2,1,0:T(1,128)} %broadcast_in_dim.6), calls=%async_computation | async-start | bytes 98304 | tf_op jit(solution)/shard_map/all_to_all | solution.py:16
where the time goes:
time: 117 us
  blocking collectives  88 us (75%)
  starting transfers between devices  12 us (10%)
  local copies, waits for them, and re-layouts  7.5 us (6%)
  waiting for transfers between devices  4.87 us (4%)
  other arithmetic  2.5 us (2%)
  matrix products  2.2 us (2%)
    all_to_all x2, blocking collectives, copy_for_each(): lax.all_to_all(jnp.broadcast_to(shard[None], (devices, *shard.shape)), ax...  64.9 us
    all_to_all x1, blocking collectives, summed_on_arrival(): lax.all_to_all(parts, axis, split_axis=0, concat_axis=0, tiled=True)  23.1 us
    all_to_all x1, starting transfers between devices, copy_for_each(): lax.all_to_all(jnp.broadcast_to(shard[None], (devices, *shard.shape)), ax...  12 us
    all_to_all x1, waiting for transfers between devices, copy_for_each(): lax.all_to_all(jnp.broadcast_to(shard[None], (devices, *shard.shape)), ax...  4.87 us
    slice x4, local copies, waits for them, and re-layouts, shards(): attended = attend(summed[:, 0], summed[:, 1], summed[:, 2])  3.81 us
    unnamed x7, local copies, waits for them, and re-layouts  2.5 us
  transfers between devices with their start and end apart: 1, of which 1 were waited for; matrix products, arithmetic and copies ran while one was open for 2% of the time, Pallas kernels for 0%

commit v1 on v0

v1 whole, which is shorter than its diff:
```python
import math

import jax
import jax.numpy as jnp
from jax import lax
from jax.experimental import pallas as pl
from jax.experimental.pallas import tpu as pltpu
from jax.sharding import PartitionSpec as P

K = 128
EPSILON = 1e-05
EXTRA = 128
HALF = 64
LIMIT = pltpu.CompilerParams(vmem_limit_bytes=20 * 2**20)


def rounded(a):
    return a.astype(jnp.bfloat16).astype(jnp.float32)


def dot32(a, b):
    return jnp.dot(a, b, preferred_element_type=jnp.float32)


def partial_kernel(devices, x_ref, g_ref, w_ref, o_ref):
    tokens, width = x_ref.shape
    columns = w_ref.shape[2]
    values = x_ref[...].astype(jnp.float32)
    middle = rounded(jnp.sum(values, axis=1, keepdims=True) / width)
    centered = values - middle
    total = jnp.sum(centered, axis=1, keepdims=True)
    square = jnp.sum(centered * centered, axis=1, keepdims=True)
    gain = g_ref[...]
    scaled = (centered * gain).astype(jnp.bfloat16)
    high = rounded(gain)
    line = lax.broadcasted_iota(jnp.int32, (16, width), 0)
    gains = jnp.where(line == 0, high, jnp.where(line == 1, gain - high, 0.0)).astype(jnp.bfloat16)
    per = tokens // devices
    row = lax.broadcasted_iota(jnp.int32, (per, EXTRA), 0)
    sums = jnp.zeros((per, EXTRA), jnp.float32)
    chunk = 0
    chunks = 3 * columns // EXTRA
    for part in range(3):
        weight = w_ref[part]
        o_ref[:, part * columns : (part + 1) * columns] = dot32(scaled, weight).astype(jnp.bfloat16)
        c = jnp.sum(dot32(gains, weight), axis=0, keepdims=True)
        for at in range(0, columns, EXTRA):
            piece = c[:, at : at + EXTRA]
            sums = jnp.where(row == chunk, piece, sums)
            sums = jnp.where(row == chunks + chunk, pltpu.roll(piece, HALF, 1), sums)
            chunk += 1
    lane = lax.broadcasted_iota(jnp.int32, (tokens, EXTRA), 1)
    extra = jnp.concatenate([sums] * devices, axis=0)
    for at, column in enumerate(
        (middle, rounded(total), total - rounded(total), rounded(square), square - rounded(square))
    ):
        extra = jnp.where(lane == at, column, extra)
    o_ref[:, 3 * columns :] = extra.astype(jnp.bfloat16)


def norm_kernel(width, r_ref, o_ref):
    devices, per, _ = r_ref.shape
    columns = o_ref.shape[1]
    chunks = columns // EXTRA
    extras = [r_ref[d, :, columns:].astype(jnp.float32) for d in range(devices)]
    middles = [e[:, 0:1] for e in extras]
    totals = [e[:, 1:2] + e[:, 2:3] for e in extras]
    squares = [e[:, 3:4] + e[:, 4:5] for e in extras]
    average = sum(m + t / width for m, t in zip(middles, totals)) / devices
    shifts = [m - average for m in middles]
    variance = sum(
        q + 2.0 * s * t + width * (s * s) for q, s, t in zip(squares, shifts, totals)
    ) / (width * devices)
    scale = lax.rsqrt(variance + EPSILON)
    wide = [jnp.broadcast_to(s, (per, EXTRA)) for s in shifts]
    turned = [pltpu.roll(e, HALF, 1) for e in extras]
    upper = lax.broadcasted_iota(jnp.int32, (1, EXTRA), 1) >= HALF
    for at in range(chunks):
        running = jnp.zeros((per, EXTRA), jnp.float32)
        for d in range(devices):
            c = jnp.where(
                upper, extras[d][at : at + 1], turned[d][chunks + at : chunks + at + 1]
            )
            term = r_ref[d, :, at * EXTRA : (at + 1) * EXTRA].astype(jnp.float32)
            running = running + term + wide[d] * c
        o_ref[:, at * EXTRA : (at + 1) * EXTRA] = (running * scale).astype(jnp.bfloat16)


def attend_kernel(x_ref, w_ref, o_ref):
    columns = w_ref.shape[0]
    scaling = 1.0 / math.sqrt(K)
    outs = []
    for at in range(0, columns, K):
        q = x_ref[:, at : at + K]
        k = x_ref[:, columns + at : columns + at + K]
        v = x_ref[:, 2 * columns + at : 2 * columns + at + K]
        scores = (
            lax.dot_general(q, k, (((1,), (1,)), ((), ())), preferred_element_type=jnp.float32)
            * scaling
        )
        largest = jnp.max(scores, axis=1, keepdims=True)
        exponent = jnp.exp(scores - largest)
        inverse = 1.0 / jnp.sum(exponent, axis=1, keepdims=True)
        outs.append(dot32((exponent * inverse).astype(jnp.bfloat16), v).astype(jnp.bfloat16))
    attended = jnp.concatenate(outs, axis=1)
    o_ref[...] = dot32(attended, w_ref[...]).astype(jnp.bfloat16)


def exchange(a, axis):
    return lax.all_to_all(a, axis, 0, 0, tiled=True)


def spread(a, axis):
    devices = lax.axis_size(axis)
    return exchange(jnp.broadcast_to(a[None], (devices, *a.shape)), axis)


def shards(tokens, norm_gain, qkv_weight, out_weight):
    count, width = tokens.shape
    columns = qkv_weight.shape[2]
    rows = lax.axis_size("row")
    cols = lax.axis_size("col")
    payload = pl.pallas_call(
        lambda *refs: partial_kernel(rows, *refs),
        out_shape=jax.ShapeDtypeStruct((count, 3 * columns + EXTRA), jnp.bfloat16),
        name="partial",
        compiler_params=LIMIT,
    )(tokens, norm_gain.reshape(1, width), jnp.transpose(qkv_weight, (1, 0, 2)))
    arrived = exchange(payload.reshape(rows, count // rows, 3 * columns + EXTRA), "row")
    own = pl.pallas_call(
        lambda *refs: norm_kernel(width, *refs),
        out_shape=jax.ShapeDtypeStruct((count // rows, 3 * columns), jnp.bfloat16),
        name="norm",
        compiler_params=LIMIT,
    )(arrived)
    qkv = spread(own, "row").reshape(count, 3 * columns)
    partial_out = pl.pallas_call(
        attend_kernel,
        out_shape=jax.ShapeDtypeStruct((count, width), jnp.bfloat16),
        name="attend",
        compiler_params=LIMIT,
    )(qkv, out_weight)
    terms = exchange(partial_out.reshape(cols, count // cols, width), "col")
    done = jnp.sum(terms.astype(jnp.float32), axis=0).astype(jnp.bfloat16)
    return spread(done, "col").reshape(count, width)


def solution(mesh):
    in_specs = (P("dp", "row"), P("row"), P("row", None, "col"), P("col", "row"))
    out_specs = P("dp", "row")
    return jax.shard_map(shards, mesh=mesh, in_specs=in_specs, out_specs=out_specs, check_vma=False)
```

time: 117 us -> 96.2 us (0.82)
  starting transfers between devices: 12 us -> 0 us
  waiting for transfers between devices: 4.87 us -> 0 us
  local copies, waits for them, and re-layouts: 7.5 us -> 3.62 us
  Pallas kernels: 0 us -> 3.85 us
  other arithmetic: 2.5 us -> 0.04 us
  matrix products: 2.2 us -> 0 us
    all_to_all x1 -> x0, starting transfers between devices: 12 us -> none  [copy_for_each(): lax.all_to_all(jnp.broadcast_to(shard[None], (devices, *shard.shape)), ax...]
    all_to_all x1 -> x0, waiting for transfers between devices: 4.87 us -> none  [copy_for_each(): lax.all_to_all(jnp.broadcast_to(shard[None], (devices, *shard.shape)), ax...]
    pallas_call x0 -> x3, Pallas kernels: none -> 3.85 us  [the longest x1 1.66 us: shards(): pl.pallas_call(attend_kernel, out_shape=jax.ShapeDtypeStruct((count, widt...]
    slice x4 -> x0, local copies, waits for them, and re-layouts: 3.81 us -> none  [shards(): attended = attend(summed[:, 0], summed[:, 1], summed[:, 2])]
    reduce_sum x4 -> x1, other arithmetic: 2.48 us -> 0.04 us  [shards(): done = jnp.sum(terms.astype(jnp.float32), axis=0).astype(jnp.bfloat16)]
    dot_general x3 -> x0, matrix products: 1.44 us -> none  [the longest x1 0.71 us: shards(): jnp.dot(normed, qkv_weight.reshape(block_width, 3 * head_columns), prefer...]
    all_to_all x3 -> x4, blocking collectives: 88 us -> 88.3 us  [exchange(): return lax.all_to_all(a, axis, 0, 0, tiled=True)]
  transfers between devices with their start and end apart: 1 -> 0, of which waited for: 1 -> 0; matrix products, arithmetic and copies ran while one was open for 2% -> 0% of each run, Pallas kernels for 0% -> 0%
where the time goes in v1:
time: 96.2 us; the launch traced here: 95.9 us
  blocking collectives  88.3 us (92%)
  Pallas kernels  3.85 us (4%)
  local copies, waits for them, and re-layouts  3.62 us (4%)
    all_to_all x4, blocking collectives, exchange(): return lax.all_to_all(a, axis, 0, 0, tiled=True)  88.3 us
    unnamed x7, local copies, waits for them, and re-layouts  2.85 us

profile of v1, /device:TPU:1, one launch (start us, length us, event | category | flops | bytes accessed | tf_op | source)
XLA Modules:
  0.0 95.9 jit_solution(13036504428142824983)
XLA Ops:
  0.0 0.7 reshape.17.refs_1_
  0.7 0.0 copy-start
  0.7 1.2 %copy-done = bf16[384,3,384]{2,0,1:T(8,128)(2,1)S(1)} copy-done((bf16[384,3,384]{2,0,1:T(8,128)(2,1)S(1)}, bf16[384,3,384]{2,0,1:T(8,128)(2,1)}, u32[]{:S(2)}) %copy-start) | copy-done | bytes 884760
  1.9 0.0 copy-start.1
  1.9 1.0 %copy-done.1 = bf16[384,384]{1,0:T(8,128)(2,1)S(1)} copy-done((bf16[384,384]{1,0:T(8,128)(2,1)S(1)}, bf16[384,384]{1,0:T(8,128)(2,1)}, u32[]{:S(2)}) %copy-start.1) | copy-done | bytes 294936
  2.8 1.0 %partial.1 = bf16[384,1280]{1,0:T(8,128)(2,1)S(1)} custom-call(bf16[384,384]{1,0:T(8,128)(2,1)S(1)} %copy-done.1, f32[1,384]{1,0:T(1,128)S(1)} %reshape.17.refs_1_, bf16[3,384,384]{2,1,0:T(8,128)(2,1)S(1)} %bitcast.8), custom_call_target="tpu_custom_call" | custom-call | tf_op jit(solution)/shard_map/partial/pallas_call | solution.py:123
  3.9 34.7 %all_to_all.20.refs_0_ = bf16[16,24,1280]{2,1,0:T(8,128)(2,1)S(1)} all-to-all(bf16[16,24,1280]{2,1,0:T(8,128)(2,1)S(1)} %bitcast.5), channel_id=1, replica_groups=mesh['row'=16,'col'=8,'dp'=4] {'row'}, dimensions={0} | all-to-all | bytes 1966080 | tf_op jit(solution)/shard_map/all_to_all | solution.py:110
  38.6 1.2 %norm.1 = bf16[24,1152]{1,0:T(8,128)(2,1)S(1)} custom-call(bf16[16,24,1280]{2,1,0:T(8,128)(2,1)S(1)} %all_to_all.20.refs_0_), custom_call_target="tpu_custom_call" | custom-call | tf_op jit(solution)/shard_map/norm/pallas_call | solution.py:130
  39.7 0.1 broadcast_in_dim.4
  39.8 0.0 copy-start.2
  39.8 29.2 %all_to_all.21 = bf16[16,24,1152]{2,1,0:T(8,128)(2,1)S(1)} all-to-all(bf16[16,24,1152]{2,1,0:T(8,128)(2,1)S(1)} %broadcast_in_dim.4), channel_id=1, replica_groups=mesh['row'=16,'col'=8,'dp'=4] {'row'}, dimensions={0} | all-to-all | bytes 1769472 | tf_op jit(solution)/shard_map/all_to_all | solution.py:110
  69.0 0.0 copy-done.2
  69.0 1.7 %attend.1 = bf16[384,384]{1,0:T(8,128)(2,1)S(1)} custom-call(bf16[384,1152]{1,0:T(8,128)(2,1)S(1)} %bitcast.6, bf16[384,384]{1,0:T(8,128)(2,1)S(1)} %copy-done.2), custom_call_target="tpu_custom_call" | custom-call | tf_op jit(solution)/shard_map/attend/pallas_call | solution.py:137
  70.7 14.2 %all_to_all.22 = bf16[8,48,384]{2,1,0:T(8,128)(2,1)S(1)} all-to-all(bf16[8,48,384]{2,1,0:T(8,128)(2,1)S(1)} %bitcast.7), channel_id=1, replica_groups=mesh['row'=16,'col'=8,'dp'=4] {'col'}, dimensions={0} | all-to-all | bytes 589824 | tf_op jit(solution)/shard_map/all_to_all | solution.py:110
  84.9 10.2 %all_to_all.23 = bf16[8,48,384]{2,1,0:T(8,128)(2,1)S(1)} all-to-all(bf16[8,48,384]{2,1,0:T(8,128)(2,1)S(1)} %broadcast_in_dim.5), channel_id=1, replica_groups=mesh['row'=16,'col'=8,'dp'=4] {'col'}, dimensions={0} | all-to-all | bytes 589824 | tf_op jit(solution)/shard_map/all_to_all | solution.py:110
  95.2 0.7 copy.6
  (2 shorter events, 0.1 us)
Async XLA Ops:
  0.7 1.2 %copy-start = (bf16[384,3,384]{2,0,1:T(8,128)(2,1)S(1)}, bf16[384,3,384]{2,0,1:T(8,128)(2,1)}, u32[]{:S(2)}) copy-start(bf16[384,3,384]{2,0,1:T(8,128)(2,1)} %param.6) | copy-start | bytes 2654212
  1.9 1.0 %copy-start.1 = (bf16[384,384]{1,0:T(8,128)(2,1)S(1)}, bf16[384,384]{1,0:T(8,128)(2,1)}, u32[]{:S(2)}) copy-start(bf16[384,384]{1,0:T(8,128)(2,1)} %refs_0_.1) | copy-start | bytes 884740
  39.8 29.2 %copy-start.2 = (bf16[384,384]{1,0:T(8,128)(2,1)S(1)}, bf16[384,384]{1,0:T(8,128)(2,1)}, u32[]{:S(2)}) copy-start(bf16[384,384]{1,0:T(8,128)(2,1)} %w_ref.1) | copy-start | bytes 884740
